TPU v7x, 32 devices: a whole 2x2x4 slice. The times are simulated.
32 devices in a mesh: group: 2 (over core), dom: 16 (over z, y, x).
Axes of the slice: x: 2, y: 2, z: 4, core: 2. Of those that a mesh axis runs over, the one named last changes fastest.
Arguments:
- nodes: bfloat16 [2, 16384, 512], P('group', 'dom'), may hold values from -6 to 6
- edges: bfloat16 [2, 32768, 512], P('group', 'dom'), may hold values from -6 to 6
- node_cotangent: bfloat16 [2, 16384, 512], P('group', 'dom'), may hold values from -6 to 6
- edge_cotangent: bfloat16 [2, 32768, 512], P('group', 'dom'), may hold values from -6 to 6
- senders: int32 [2, 32768], P('group', 'dom'), may hold values from 0 to 1151, as said below
- receivers: int32 [2, 32768], P('group', 'dom'), may hold values from 0 to 1023
- send_rows: int32 [2, 256, 8], P('group', 'dom'), may hold values from 0 to 1023
- edge_in: bfloat16 [1536, 512], replicated, may hold values from -0.15625 to 0.15625
- edge_out: bfloat16 [512, 512], replicated, may hold values from -0.25 to 0.25
- edge_gain: float32 [512], replicated, may hold values from 0.1 to 1.9
- node_in: bfloat16 [1024, 512], replicated, may hold values from -0.1875 to 0.1875
- node_out: bfloat16 [512, 512], replicated, may hold values from -0.25 to 0.25
- node_gain: float32 [512], replicated, may hold values from 0.1 to 1.9
Outputs:
- grad_edges: bfloat16 [2, 32768, 512], P('group', 'dom')
- grad_nodes: bfloat16 [2, 16384, 512], P('group', 'dom')
- grad_edge_in: float32 [1536, 512], P('dom')
- grad_edge_out: float32 [512, 512], P('dom')
- grad_node_in: float32 [1024, 512], P('dom')
- grad_node_out: float32 [512, 512], P('dom')
- grad_edge_gain: float32 [512], P('dom')
- grad_node_gain: float32 [512], P('dom')
Inputs may be any that keep to these rules, and one draw needn't show every extreme that they name: `senders`: an id below 1024 is a row of the edge's own partition; an id 1024 + p * 8 + s is slot s of the list partition p of the same graph sends to the edge's partition. The slots read from one peer lie below a count of that edge's partition and peer, and on every partition some peer's slot 7 is read.
All inputs are finite; a program needn't handle non-finite values.
Results may differ from a plain program's by a relative error of at most 0.019.
Values may be sent and summed in bfloat16 or wider, within the bound.
A program may use at most 128 MiB of HBM per device.

v0:
```python
import functools

import jax
import jax.numpy as jnp
from jax import lax
from jax.experimental import pallas as pl
from jax.experimental.pallas import tpu as pltpu
from jax.sharding import PartitionSpec as P

MESH = pl.DeviceIdType.MESH
F32 = jnp.float32
BF16 = jnp.bfloat16
I32 = jnp.int32
LANES = 128


def dot(first, second):
    return jnp.dot(first, second, preferred_element_type=F32)


def dot_tn(first, second):
    return lax.dot_general(first, second, (((0,), (0,)), ((), ())), preferred_element_type=F32)


def dot_nt(first, second):
    return lax.dot_general(first, second, (((1,), (1,)), ((), ())), preferred_element_type=F32)


def normalize(hidden):
    centre = hidden - jnp.mean(hidden, axis=-1, keepdims=True)
    inverse = lax.rsqrt(jnp.mean(centre * centre, axis=-1, keepdims=True) + 1e-05)
    return centre * inverse, inverse


def norm_back(upstream, gain, normed, inverse):
    scaled = upstream * gain
    return inverse * (
        scaled
        - jnp.mean(scaled, axis=-1, keepdims=True)
        - normed * jnp.mean(scaled * normed, axis=-1, keepdims=True)
    )


def swish_pair(value):
    logistic = jax.nn.sigmoid(value)
    return value * logistic, logistic * (1.0 + value * (1.0 - logistic))


def hot(mask):
    return jnp.where(mask, 1.0, 0.0).astype(BF16)


def pick_rows(column, base, count):
    lane = lax.broadcasted_iota(I32, column.shape, 1)
    return jnp.concatenate(
        [hot(column == lane + (base + block)) for block in range(0, count, LANES)], axis=1
    )


def pick_columns(row, base, count):
    index = lax.broadcasted_iota(I32, (count, row.shape[1]), 0) + base
    return hot(index == row)


def fold(value):
    return jnp.sum(value.reshape(value.shape[0] // 8, 8, value.shape[1]), axis=0)


def tile_of(count, sizes):
    return next(size for size in sizes if count % size == 0)


class Chunk:
    def __init__(self, env, mat, out, start, wide, refs):
        self.env, self.mat, self.out, self.start, self.wide = env, mat, out, start, wide
        (
            self.from_graph, self.sum_graph, self.from_plane, self.sum_plane, self.from_layer,
            self.total, self.from_other, self.sem,
        ) = refs
        self.slot = 0

    def send(self, src, dst, device):
        slot = self.slot
        self.slot += 1
        return self.env.send(src, dst, self.sem.at[0, slot], self.sem.at[1, slot], device)

    def columns(self, group):
        return pl.ds(pl.multiple_of(self.start + group * self.wide, LANES), self.wide)

    def graph(self):
        env = self.env
        self.graph_copy = self.send(
            self.mat.at[:, self.columns(env.other)], self.from_graph, (env.other, env.dom)
        )

    def planes(self):
        env = self.env
        self.graph_copy.wait_recv()
        value = self.mat[:, self.columns(env.group)].astype(F32) + self.from_graph[...].astype(F32)
        self.sum_graph[...] = value.astype(BF16).reshape(self.sum_graph.shape)
        self.rows = self.from_layer.shape[1]
        self.plane_copies = []
        for step in range(1, env.planes):
            target = lax.rem(env.plane + step, env.planes)
            self.plane_copies.append(
                self.send(
                    self.sum_graph.at[:, target],
                    self.from_plane.at[step - 1],
                    (env.group, env.layer * env.planes + target),
                )
            )

    def layers(self):
        env = self.env
        value = self.sum_graph[:, env.plane].astype(F32)
        for step in range(1, env.planes):
            self.plane_copies[step - 1].wait_recv()
            value = value + self.from_plane[step - 1].astype(F32)
        self.sum_plane[...] = value.astype(BF16)
        self.layer_copies = []
        for step in range(1, env.layers):
            target = lax.rem(env.layer + step, env.layers)
            self.layer_copies.append(
                self.send(
                    self.sum_plane.at[target],
                    self.from_layer.at[step - 1],
                    (env.group, target * env.planes + env.plane),
                )
            )

    def finish(self):
        env = self.env
        value = self.sum_plane[env.layer].astype(F32)
        for step in range(1, env.layers):
            self.layer_copies[step - 1].wait_recv()
            value = value + self.from_layer[step - 1].astype(F32)
        short = value.astype(BF16)
        self.total[...] = short
        self.other_copy = self.send(self.total, self.from_other, (env.other, env.dom))
        self.out[:, self.columns(env.group)] = short.astype(F32)

    def place(self):
        self.other_copy.wait_recv()
        self.out[:, self.columns(self.env.other)] = self.from_other[...].astype(F32)


class Env:
    pass


def layer_kernel(shape, *refs):
    node_count, edge_count, width, domains, slots, planes, layers, plan = shape
    halo = domains * slots
    rows_all = node_count + halo
    inputs, refs = refs[:13], refs[13:]
    (edges_out, nodes_out, ein_out, eout_out, nin_out, nout_out, gain_out), refs = refs[:7], refs[7:]
    loaded, refs = refs[:13], refs[13:]
    (
        nodes, edges, ncot, ecot, send_row, recv_row, list_in, ein, eout, egain, nin, nout, ngain,
    ) = loaded
    (
        send_col, recv_col, list_col, outgoing, arrived, from_table, to_table, halo_table,
        edge_pre, edge_slope, edge_act, edge_hat, edge_inv, edge_mid, edge_grad,
        gathered, node_act, node_mid, node_grad, gathered_grad, sums_from, sums_to, returning, returned,
        ein_grad, eout_grad, nin_grad, nout_grad,
        gains, gain_graph, gain_mine, gain_plane, gain_mid, gain_layer,
        load_sem, halo_sem, back_sem, gain_sem,
    ), refs = refs[:38], refs[38:]

    env = Env()
    env.group = lax.axis_index("group")
    env.dom = lax.axis_index("dom")
    env.other = 1 - env.group
    env.planes, env.layers = planes, layers
    env.layer = env.dom // planes
    env.plane = lax.rem(env.dom, planes)
    sent = []

    def send(src, dst, send_sem, recv_sem, device):
        copy = pltpu.make_async_remote_copy(
            src_ref=src, dst_ref=dst, send_sem=send_sem, recv_sem=recv_sem,
            device_id=device, device_id_type=MESH,
        )
        copy.start()
        sent.append(copy)
        return copy

    env.send = send

    def peer(step):
        return lax.rem(env.dom + step, domains)

    loads = [
        pltpu.make_async_copy(src, dst, load_sem.at[index])
        for index, (src, dst) in enumerate(zip(inputs, loaded))
    ]
    NODES, EDGES, NCOT, ECOT, SEND, RECV, LIST, EIN, EOUT, EGAIN, NIN, NOUT, NGAIN = range(13)
    for index in (LIST, NODES, SEND, RECV, EIN, EDGES, EOUT, EGAIN, NIN, NOUT, NGAIN, NCOT, ECOT):
        loads[index].start()

    barrier = pltpu.get_barrier_semaphore()
    pl.semaphore_signal(barrier, inc=1, device_id=(env.other, env.dom), device_id_type=MESH)
    for step in range(1, domains):
        pl.semaphore_signal(barrier, inc=1, device_id=(env.group, peer(step)), device_id_type=MESH)

    loads[LIST].wait()
    for index in range(domains):
        list_col[index * slots : (index + 1) * slots, :] = jnp.broadcast_to(
            list_in[:, index : index + 1], (slots, LANES)
        )
    loads[NODES].wait()
    outgoing[...] = (
        dot(pick_rows(list_col[...], 0, node_count), nodes[...])
        .astype(BF16)
        .reshape(domains, slots, width)
    )
    pl.semaphore_wait(barrier, domains)
    halo_copies = [
        send(
            outgoing.at[peer(step)],
            arrived.at[env.dom],
            halo_sem.at[0, step - 1],
            halo_sem.at[1, step - 1],
            (env.group, peer(step)),
        )
        for step in range(1, domains)
    ]
    arrived[env.dom] = outgoing[env.dom]

    loads[SEND].wait()
    loads[RECV].wait()

    @pl.loop(0, edge_count // LANES)
    def _(index):
        place = pl.ds(pl.multiple_of(index * LANES, LANES), LANES)
        send_col[place, :] = jnp.transpose(jnp.broadcast_to(send_row[:, place], (LANES, LANES)))
        recv_col[place, :] = jnp.transpose(jnp.broadcast_to(recv_row[:, place], (LANES, LANES)))

    loads[EIN].wait()
    own_w = slice(0, width)
    from_w = slice(width, 2 * width)
    to_w = slice(2 * width, 3 * width)
    step_n = tile_of(node_count, (512, 256, 128))

    @pl.loop(0, node_count // step_n)
    def _(index):
        place = pl.ds(pl.multiple_of(index * step_n, step_n), step_n)
        from_table[place, :] = dot(nodes[place, :], ein[from_w, :]).astype(BF16)
        to_table[place, :] = dot(nodes[place, :], ein[to_w, :]).astype(BF16)

    loads[EDGES].wait()
    step_e = tile_of(edge_count, (256, 128))

    @pl.loop(0, edge_count // step_e)
    def _(index):
        place = pl.ds(pl.multiple_of(index * step_e, step_e), step_e)
        edge_pre[place, :] = (
            dot(edges[place, :], ein[own_w, :])
            + dot(pick_rows(send_col[place, :], 0, node_count), from_table[...])
            + dot(pick_rows(recv_col[place, :], 0, node_count), to_table[...])
        )

    loads[EOUT].wait()
    loads[EGAIN].wait()
    for copy in halo_copies:
        copy.wait_recv()
    halo_table[...] = dot(arrived[...].reshape(halo, width), ein[from_w, :]).astype(BF16)

    @pl.loop(0, edge_count // step_e)
    def _(index):
        place = pl.ds(pl.multiple_of(index * step_e, step_e), step_e)
        value = edge_pre[place, :] + dot(
            pick_rows(send_col[place, :], node_count, halo), halo_table[...]
        )
        act, slope = swish_pair(value)
        act = act.astype(BF16)
        edge_act[place, :] = act
        edge_slope[place, :] = slope
        normed, inverse = normalize(dot(act, eout[...]))
        edge_hat[place, :] = normed
        edge_inv[place, :] = jnp.broadcast_to(inverse, (step_e, LANES))
        edge_mid[place, :] = (normed * egain[...]).astype(BF16)

    for index in (NIN, NOUT, NGAIN, NCOT):
        loads[index].wait()
    near = slice(0, width)
    far = slice(width, 2 * width)
    gains[...] = jnp.zeros_like(gains)
    step_v = tile_of(node_count, (256, 128))

    @pl.loop(0, node_count // step_v)
    def _(index):
        start = pl.multiple_of(index * step_v, step_v)
        place = pl.ds(start, step_v)
        got = dot(pick_columns(recv_row[...], start, step_v), edge_mid[...]).astype(BF16)
        gathered[place, :] = got
        act, slope = swish_pair(dot(nodes[place, :], nin[near, :]) + dot(got, nin[far, :]))
        act = act.astype(BF16)
        node_act[place, :] = act
        normed, inverse = normalize(dot(act, nout[...]))
        upstream = ncot[place, :].astype(F32)
        gains[8:16, :] += fold(upstream * normed)
        post = norm_back(upstream, ngain[...], normed, inverse).astype(BF16)
        node_mid[place, :] = post
        grad = (dot_nt(post, nout[...]) * slope).astype(BF16)
        node_grad[place, :] = grad
        gathered_grad[place, :] = dot_nt(grad, nin[far, :]).astype(BF16)

    chunks = {}
    mats = {"ein": ein_grad, "eout": eout_grad, "nin": nin_grad, "nout": nout_grad}
    outs = {"ein": ein_out, "eout": eout_out, "nin": nin_out, "nout": nout_out}
    for index, (name, start, wide) in enumerate(plan):
        chunks[name, start] = Chunk(
            env, mats[name], outs[name], start, wide, refs[index * 8 : (index + 1) * 8]
        )
    half = width // 2
    nout_c, nin_c, eout_c = chunks["nout", 0], chunks["nin", 0], chunks["eout", 0]
    ein_c = (chunks["ein", 0], chunks["ein", half])

    nout_grad[...] = dot_tn(node_act[...], node_mid[...]).astype(BF16)
    nout_c.graph()
    nin_grad[near, :] = dot_tn(nodes[...], node_grad[...]).astype(BF16)
    nin_grad[far, :] = dot_tn(gathered[...], node_grad[...]).astype(BF16)
    nin_c.graph()

    loads[ECOT].wait()

    @pl.loop(0, edge_count // step_e)
    def _(index):
        place = pl.ds(pl.multiple_of(index * step_e, step_e), step_e)
        upstream = ecot[place, :].astype(F32) + dot(
            pick_rows(recv_col[place, :], 0, node_count), gathered_grad[...]
        )
        normed = edge_hat[place, :]
        gains[0:8, :] += fold(upstream * normed)
        edge_mid[place, :] = norm_back(
            upstream, egain[...], normed, edge_inv[place, 0:1]
        ).astype(BF16)

    nout_c.planes()
    nin_c.planes()
    gains[0:1, :] = jnp.sum(gains[0:8, :], axis=0, keepdims=True)
    gains[1:2, :] = jnp.sum(gains[8:16, :], axis=0, keepdims=True)
    gain_graph_copy = send(
        gains.at[0:8], gain_graph, gain_sem.at[0, 0], gain_sem.at[1, 0], (env.other, env.dom)
    )

    eout_grad[...] = dot_tn(edge_act[...], edge_mid[...]).astype(BF16)
    eout_c.graph()

    gain_graph_copy.wait_recv()
    gain_mine[...] = gains[0:8, :] + gain_graph[...]
    gain_copies = [
        send(
            gain_mine, gain_plane.at[step - 1], gain_sem.at[0, step], gain_sem.at[1, step],
            (env.group, env.layer * planes + lax.rem(env.plane + step, planes)),
        )
        for step in range(1, planes)
    ]

    @pl.loop(0, edge_count // step_e)
    def _(index):
        place = pl.ds(pl.multiple_of(index * step_e, step_e), step_e)
        edge_grad[place, :] = (
            dot_nt(edge_mid[place, :], eout[...]) * edge_slope[place, :]
        ).astype(BF16)

    nout_c.layers()
    nin_c.layers()
    eout_c.planes()
    total = gain_mine[...]
    for step in range(1, planes):
        gain_copies[step - 1].wait_recv()
        total = total + gain_plane[step - 1]
    gain_mid[...] = total
    gain_copies = [
        send(
            gain_mid, gain_layer.at[step - 1],
            gain_sem.at[0, planes + step - 1], gain_sem.at[1, planes + step - 1],
            (env.group, lax.rem(env.layer + step, layers) * planes + env.plane),
        )
        for step in range(1, layers)
    ]

    step_s = tile_of(rows_all, (384, 256, 128))
    step_t = tile_of(node_count, (256, 128))

    def scatter_from(columns):
        @pl.loop(0, rows_all // step_s)
        def _(index):
            start = pl.multiple_of(index * step_s, LANES)
            sums_from[pl.ds(start, step_s), columns] = dot(
                pick_columns(send_row[...], start, step_s), edge_grad[:, columns]
            ).astype(BF16)

    def scatter_to(columns):
        @pl.loop(0, node_count // step_t)
        def _(index):
            start = pl.multiple_of(index * step_t, step_t)
            sums_to[pl.ds(start, step_t), columns] = dot(
                pick_columns(recv_row[...], start, step_t), edge_grad[:, columns]
            ).astype(BF16)

    def edge_in_grads(columns):
        ein_grad[own_w, columns] = dot_tn(edges[...], edge_grad[:, columns]).astype(BF16)
        ein_grad[from_w, columns] = (
            dot_tn(nodes[...], sums_from[0:node_count, columns])
            + dot_tn(arrived[...].reshape(halo, width), sums_from[node_count:rows_all, columns])
        ).astype(BF16)
        ein_grad[to_w, columns] = dot_tn(nodes[...], sums_to[:, columns]).astype(BF16)

    first, second = slice(0, half), slice(half, width)
    scatter_from(first)
    scatter_to(first)
    edge_in_grads(first)
    ein_c[0].graph()
    nout_c.finish()
    nin_c.finish()
    eout_c.layers()

    scatter_from(second)
    returning[...] = (
        dot_nt(sums_from[node_count:rows_all, :], ein[from_w, :])
        .astype(BF16)
        .reshape(domains, slots, width)
    )
    back_copies = [
        send(
            returning.at[peer(step)],
            returned.at[env.dom],
            back_sem.at[0, step - 1],
            back_sem.at[1, step - 1],
            (env.group, peer(step)),
        )
        for step in range(1, domains)
    ]
    returned[env.dom] = returning[env.dom]
    ein_c[0].planes()
    scatter_to(second)
    edge_in_grads(second)
    ein_c[1].graph()
    nout_c.place()
    nin_c.place()
    eout_c.finish()
    ein_c[0].layers()

    total = gain_mid[...]
    for step in range(1, layers):
        gain_copies[step - 1].wait_recv()
        total = total + gain_layer[step - 1]
    gain_out[...] = total

    def edge_tail(begin, end):
        @pl.loop(begin, end)
        def _(index):
            place = pl.ds(pl.multiple_of(index * step_e, step_e), step_e)
            edges_out[place, :] = (
                ecot[place, :].astype(F32) + dot_nt(edge_grad[place, :], ein[own_w, :])
            ).astype(BF16)

    blocks = edge_count // step_e
    edge_tail(0, blocks // 2)
    ein_c[1].planes()
    eout_c.place()
    edge_tail(blocks // 2, blocks)
    ein_c[0].finish()

    for step in range(1, domains):
        back_copies[step - 1].wait_recv()

    list_row = jnp.concatenate(
        [
            jnp.transpose(list_col[block : block + LANES, :])[0:1, :]
            for block in range(0, halo, LANES)
        ],
        axis=1,
    )
    back = returned[...].reshape(halo, width)

    def node_tail(begin, end):
        @pl.loop(begin, end)
        def _(index):
            start = pl.multiple_of(index * step_v, step_v)
            place = pl.ds(start, step_v)
            nodes_out[place, :] = (
                ncot[place, :].astype(F32)
                + dot_nt(node_grad[place, :], nin[near, :])
                + dot_nt(sums_from[place, :], ein[from_w, :])
                + dot_nt(sums_to[place, :], ein[to_w, :])
                + dot(pick_columns(list_row, start, step_v), back)
            ).astype(BF16)

    blocks = node_count // step_v
    node_tail(0, blocks // 2)
    ein_c[1].layers()
    ein_c[0].place()
    node_tail(blocks // 2, blocks)
    ein_c[1].finish()
    ein_c[1].place()
    for copy in sent:
        copy.wait_send()


def layer(args, domains, planes, layers):
    nodes, edges, ncot, ecot, senders, receivers, lists, ein, eout, egain, nin, nout, ngain = args
    node_count, width = nodes.shape
    edge_count = edges.shape[0]
    slots = lists.shape[0]
    halo = domains * slots
    half = width // 2
    plan = (
        ("nout", 0, half),
        ("nin", 0, half),
        ("eout", 0, half),
        ("ein", 0, half // 2),
        ("ein", half, half // 2),
    )
    rows = {"ein": 3 * width, "eout": width, "nin": 2 * width, "nout": width}
    dma = pltpu.SemaphoreType.DMA
    vmem = pltpu.VMEM
    anywhere = pl.BlockSpec(memory_space=pl.ANY)
    inside = pl.BlockSpec(memory_space=pltpu.VMEM)
    share = {name: count // domains for name, count in rows.items()}
    out_shape = (
        jax.ShapeDtypeStruct((edge_count, width), BF16),
        jax.ShapeDtypeStruct((node_count, width), BF16),
        jax.ShapeDtypeStruct((share["ein"], width), F32),
        jax.ShapeDtypeStruct((share["eout"], width), F32),
        jax.ShapeDtypeStruct((share["nin"], width), F32),
        jax.ShapeDtypeStruct((share["nout"], width), F32),
        jax.ShapeDtypeStruct((8, width), F32),
    )
    scratch = [vmem(arg.shape, arg.dtype) for arg in args]
    scratch += [
        vmem((edge_count, LANES), I32),
        vmem((edge_count, LANES), I32),
        vmem((halo, LANES), I32),
        vmem((domains, slots, width), BF16),
        vmem((domains, slots, width), BF16),
        vmem((node_count, width), BF16),
        vmem((node_count, width), BF16),
        vmem((halo, width), BF16),
        vmem((edge_count, width), F32),
        vmem((edge_count, width), F32),
        vmem((edge_count, width), BF16),
        vmem((edge_count, width), F32),
        vmem((edge_count, LANES), F32),
        vmem((edge_count, width), BF16),
        vmem((edge_count, width), BF16),
        vmem((node_count, width), BF16),
        vmem((node_count, width), BF16),
        vmem((node_count, width), BF16),
        vmem((node_count, width), BF16),
        vmem((node_count, width), BF16),
        vmem((node_count + halo, width), BF16),
        vmem((node_count, width), BF16),
        vmem((domains, slots, width), BF16),
        vmem((domains, slots, width), BF16),
        vmem((3 * width, width), BF16),
        vmem((width, width), BF16),
        vmem((2 * width, width), BF16),
        vmem((width, width), BF16),
        vmem((16, width), F32),
        vmem((8, width), F32),
        vmem((8, width), F32),
        vmem((planes - 1, 8, width), F32),
        vmem((8, width), F32),
        vmem((layers - 1, 8, width), F32),
        dma((13,)),
        dma((2, domains - 1)),
        dma((2, domains - 1)),
        dma((2, planes + layers - 1)),
    ]
    for name, _, wide in plan:
        count = share[name]
        scratch += [
            vmem((rows[name], wide), BF16),
            vmem((layers, planes, count, wide), BF16),
            vmem((planes - 1, layers, count, wide), BF16),
            vmem((layers, count, wide), BF16),
            vmem((layers - 1, count, wide), BF16),
            vmem((count, wide), BF16),
            vmem((count, wide), BF16),
            dma((2, planes + layers)),
        ]
    shape = (node_count, edge_count, width, domains, slots, planes, layers, plan)
    return pl.pallas_call(
        functools.partial(layer_kernel, shape),
        out_shape=out_shape,
        in_specs=[anywhere] * len(args),
        out_specs=(inside,) * len(out_shape),
        scratch_shapes=scratch,
        compiler_params=pltpu.CompilerParams(
            collective_id=0, has_side_effects=True, vmem_limit_bytes=63 * 1024 * 1024
        ),
        name="layer",
    )(*args)


def local(
    nodes, edges, node_cotangent, edge_cotangent, senders, receivers, send_rows,
    edge_in, edge_out, edge_gain, node_in, node_out, node_gain,
):
    domains = lax.axis_size("dom")
    planes = 1
    while planes * planes < domains:
        planes *= 2
    width = nodes.shape[2]
    args = (
        nodes[0], edges[0], node_cotangent[0], edge_cotangent[0], senders, receivers,
        send_rows[0].T, edge_in, edge_out, edge_gain[None], node_in, node_out, node_gain[None],
    )
    results = layer(args, domains, planes, domains // planes)
    grad_edges, grad_nodes, ein, eout, nin, nout, gains = results
    share = width // domains
    own = lax.dynamic_slice_in_dim(gains, lax.axis_index("dom") * share, share, 1)
    return grad_edges[None], grad_nodes[None], ein, eout, nin, nout, own[0], own[1]


def solution(mesh):
    placed = (
        P("group", "dom", None),
        P("group", "dom", None),
        P("group", "dom", None),
        P("group", "dom", None),
        P("group", "dom"),
        P("group", "dom"),
        P("group", "dom", None),
        P(),
        P(),
        P(),
        P(),
        P(),
        P(),
    )
    return jax.shard_map(
        local,
        mesh=mesh,
        in_specs=placed,
        out_specs=(
            P("group", "dom", None),
            P("group", "dom", None),
            P("dom", None),
            P("dom", None),
            P("dom", None),
            P("dom", None),
            P("dom"),
            P("dom"),
        ),
        check_vma=False,
    )
```

profile of v0, /device:TPU:0, one launch (start us, length us, event | category | flops | bytes accessed | tf_op | source)
XLA Modules:
  0.0 85.4 jit_solution(17284770671401258018)
XLA Ops:
  0.6 76.6 %layer.1 = (bf16[2048,512]{1,0:T(8,128)(2,1)}, bf16[1024,512]{1,0:T(8,128)(2,1)}, f32[96,512]{1,0:T(8,128)}, f32[32,512]{1,0:T(8,128)}, f32[64,512]{1,0:T(8,128)}, /*index=5*/f32[32,512]{1,0:T(8,128)}, f32[8,512]{1,0:T(8,128)}) custom-call(bf16[1024,512]{1,0:T(8,128)(2,1)} %bitcast.19, bf16[2048,512]{1,0:T(8,128)(2,1)} %bitcast.16, ...), custom_call_target="tpu_custom_call" | custom-call | tf_op jit(solution)/shard_map/layer/pallas_call | solution.py:587
  77.3 0.8 constant_dynamic-slice_fusion
  78.0 0.5 slice_bitcast_fusion
  78.6 0.0 copy-start
  78.6 3.1 %copy.27 = bf16[1,2048,512]{2,1,0:T(8,128)(2,1)} copy(bf16[1,2048,512]{2,1,0:T(8,128)(2,1)} %bitcast.15) | data formatting | bytes 4194304
  81.7 0.0 copy-done
  81.7 0.0 copy-start.1
  81.7 0.0 copy-start.4
  81.7 0.0 copy-start.2
  81.7 0.0 copy-start.3
  81.7 1.0 %copy.28 = bf16[1,1024,512]{2,1,0:T(8,128)(2,1)} copy(bf16[1,1024,512]{2,1,0:T(8,128)(2,1)S(1)} %bitcast.18) | data formatting | bytes 2097152
  82.7 0.1 copy-done.1
  82.8 0.7 copy.29
  83.5 0.0 copy-done.4
  83.5 0.6 copy.30
  84.1 0.0 copy-done.2
  84.1 0.7 copy.31
  84.7 0.0 copy-done.3
  84.7 0.6 copy.32
Async XLA Ops:
  78.6 3.1 %copy-start = (bf16[1024,512]{1,0:T(8,128)(2,1)S(1)}, bf16[1024,512]{1,0:T(8,128)(2,1)}, u32[]{:S(2)}) copy-start(bf16[1024,512]{1,0:T(8,128)(2,1)} %get-tuple-element.16) | copy-start | bytes 3145732
  81.7 1.1 %copy-start.1 = (f32[96,512]{1,0:T(8,128)S(1)}, f32[96,512]{1,0:T(8,128)}, u32[]{:S(2)}) copy-start(f32[96,512]{1,0:T(8,128)} %get-tuple-element.34) | copy-start | bytes 589828
  81.7 1.7 %copy-start.4 = (f32[32,512]{1,0:T(8,128)S(1)}, f32[32,512]{1,0:T(8,128)}, u32[]{:S(2)}) copy-start(f32[32,512]{1,0:T(8,128)} %get-tuple-element.35) | copy-start | bytes 196612
  81.7 2.4 %copy-start.2 = (f32[64,512]{1,0:T(8,128)S(1)}, f32[64,512]{1,0:T(8,128)}, u32[]{:S(2)}) copy-start(f32[64,512]{1,0:T(8,128)} %get-tuple-element.36) | copy-start | bytes 393220
  81.7 3.0 %copy-start.3 = (f32[32,512]{1,0:T(8,128)S(1)}, f32[32,512]{1,0:T(8,128)}, u32[]{:S(2)}) copy-start(f32[32,512]{1,0:T(8,128)} %get-tuple-element.37) | copy-start | bytes 196612
where the time goes:
time: 85.6 us; the launch traced here: 85.4 us
  Pallas kernels  76.6 us (89%)
  local copies, waits for them, and re-layouts  8.06 us (9%)
    pallas_call x1, Pallas kernels, layer(): pl.pallas_call(functools.partial(layer_kernel, shape), out_shape=out_shap...  76.6 us
    unnamed x16, local copies, waits for them, and re-layouts  6.79 us

commit v1 on v0

--- a/solution.py
+++ b/solution.py
@@ -74,8 +74,8 @@
     def __init__(self, env, mat, out, start, wide, refs):
         self.env, self.mat, self.out, self.start, self.wide = env, mat, out, start, wide
         (
-            self.from_graph, self.sum_graph, self.from_plane, self.sum_plane, self.from_layer,
-            self.total, self.from_other, self.sem,
+            self.from_graph, self.sum_graph, self.from_first, self.sum_first, self.from_second,
+            self.sum_second, self.from_layer, self.total, self.from_other, self.sem,
         ) = refs
         self.slot = 0
 
@@ -93,36 +93,59 @@
             self.mat.at[:, self.columns(env.other)], self.from_graph, (env.other, env.dom)
         )
 
-    def planes(self):
+    def first(self):
         env = self.env
+        side = env.side
+        count = self.total.shape[0]
         self.graph_copy.wait_recv()
-        value = self.mat[:, self.columns(env.group)].astype(F32) + self.from_graph[...].astype(F32)
-        self.sum_graph[...] = value.astype(BF16).reshape(self.sum_graph.shape)
-        self.rows = self.from_layer.shape[1]
-        self.plane_copies = []
-        for step in range(1, env.planes):
-            target = lax.rem(env.plane + step, env.planes)
-            self.plane_copies.append(
+        for index in range(env.layers * side * side):
+            x, y, layer = index % side, index // side % side, index // (side * side)
+            rows = slice(index * count, (index + 1) * count)
+            value = self.mat[rows, self.columns(env.group)].astype(F32)
+            value = value + self.from_graph[rows, :].astype(F32)
+            self.sum_graph[x + env.group * (y - x), y + env.group * (x - y), layer] = value.astype(BF16)
+        self.copies = []
+        for step in range(1, side):
+            target = lax.rem(env.head + step, side)
+            self.copies.append(
                 self.send(
-                    self.sum_graph.at[:, target],
-                    self.from_plane.at[step - 1],
-                    (env.group, env.layer * env.planes + target),
+                    self.sum_graph.at[target],
+                    self.from_first.at[step - 1],
+                    (env.group, env.base + target * env.head_stride + env.tail * env.tail_stride),
                 )
             )
 
-    def layers(self):
+    def second(self):
         env = self.env
-        value = self.sum_graph[:, env.plane].astype(F32)
-        for step in range(1, env.planes):
-            self.plane_copies[step - 1].wait_recv()
-            value = value + self.from_plane[step - 1].astype(F32)
-        self.sum_plane[...] = value.astype(BF16)
-        self.layer_copies = []
+        value = self.sum_graph[env.head].astype(F32)
+        for step in range(1, env.side):
+            self.copies[step - 1].wait_recv()
+            value = value + self.from_first[step - 1].astype(F32)
+        self.sum_first[...] = value.astype(BF16)
+        self.copies = []
+        for step in range(1, env.side):
+            target = lax.rem(env.tail + step, env.side)
+            self.copies.append(
+                self.send(
+                    self.sum_first.at[target],
+                    self.from_second.at[step - 1],
+                    (env.group, env.base + env.head * env.head_stride + target * env.tail_stride),
+                )
+            )
+
+    def along(self):
+        env = self.env
+        value = self.sum_first[env.tail].astype(F32)
+        for step in range(1, env.side):
+            self.copies[step - 1].wait_recv()
+            value = value + self.from_second[step - 1].astype(F32)
+        self.sum_second[...] = value.astype(BF16)
+        self.copies = []
         for step in range(1, env.layers):
             target = lax.rem(env.layer + step, env.layers)
-            self.layer_copies.append(
+            self.copies.append(
                 self.send(
-                    self.sum_plane.at[target],
+                    self.sum_second.at[target],
                     self.from_layer.at[step - 1],
                     (env.group, target * env.planes + env.plane),
                 )
@@ -130,9 +153,9 @@
 
     def finish(self):
         env = self.env
-        value = self.sum_plane[env.layer].astype(F32)
+        value = self.sum_second[env.layer].astype(F32)
         for step in range(1, env.layers):
-            self.layer_copies[step - 1].wait_recv()
+            self.copies[step - 1].wait_recv()
             value = value + self.from_layer[step - 1].astype(F32)
         short = value.astype(BF16)
         self.total[...] = short
@@ -149,7 +172,8 @@
 
 
 def layer_kernel(shape, *refs):
-    node_count, edge_count, width, domains, slots, planes, layers, plan = shape
+    node_count, edge_count, width, domains, slots, side, layers, plan = shape
+    planes = side * side
     halo = domains * slots
     rows_all = node_count + halo
     inputs, refs = refs[:13], refs[13:]
@@ -160,20 +184,25 @@
     ) = loaded
     (
         send_col, recv_col, list_col, outgoing, arrived, from_table, to_table, halo_table,
-        edge_pre, edge_slope, edge_act, edge_hat, edge_inv, edge_mid, edge_grad,
+        even, odd, edge_slope, edge_act, edge_hat, edge_inv, edge_mid, edge_grad,
         gathered, node_act, node_mid, node_grad, gathered_grad, sums_from, sums_to, returning, returned,
         ein_grad, eout_grad, nin_grad, nout_grad,
         gains, gain_graph, gain_mine, gain_plane, gain_mid, gain_layer,
         load_sem, halo_sem, back_sem, gain_sem,
-    ), refs = refs[:38], refs[38:]
+    ), refs = refs[:39], refs[39:]
 
     env = Env()
     env.group = lax.axis_index("group")
     env.dom = lax.axis_index("dom")
     env.other = 1 - env.group
-    env.planes, env.layers = planes, layers
+    env.planes, env.layers, env.side = planes, layers, side
     env.layer = env.dom // planes
     env.plane = lax.rem(env.dom, planes)
+    env.base = env.layer * planes
+    x, y = lax.rem(env.plane, side), env.plane // side
+    env.head, env.tail = x + env.group * (y - x), y + env.group * (x - y)
+    env.head_stride = 1 + env.group * (side - 1)
+    env.tail_stride = side - env.group * (side - 1)
     sent = []
 
     def send(src, dst, send_sem, recv_sem, device):
@@ -230,9 +259,8 @@
     loads[SEND].wait()
     loads[RECV].wait()
 
-    @pl.loop(0, edge_count // LANES)
-    def _(index):
-        place = pl.ds(pl.multiple_of(index * LANES, LANES), LANES)
+    for block in range(0, edge_count, LANES):
+        place = slice(block, block + LANES)
         send_col[place, :] = jnp.transpose(jnp.broadcast_to(send_row[:, place], (LANES, LANES)))
         recv_col[place, :] = jnp.transpose(jnp.broadcast_to(recv_row[:, place], (LANES, LANES)))
 
@@ -248,28 +276,46 @@
         from_table[place, :] = dot(nodes[place, :], ein[from_w, :]).astype(BF16)
         to_table[place, :] = dot(nodes[place, :], ein[to_w, :]).astype(BF16)
 
-    loads[EDGES].wait()
+    for index in (EDGES, EOUT, EGAIN):
+        loads[index].wait()
     step_e = tile_of(edge_count, (256, 128))
 
-    @pl.loop(0, edge_count // step_e)
-    def _(index):
-        place = pl.ds(pl.multiple_of(index * step_e, step_e), step_e)
-        edge_pre[place, :] = (
+    def tile(index):
+        return pl.ds(pl.multiple_of(index * step_e, step_e), step_e)
+
+    def pipeline(begin, end, lead, follow, between=None):
+        lead(begin, even)
+        if between is not None:
+            between()
+
+        @pl.loop(0, (end - begin) // 2 - 1)
+        def _(pair):
+            index = begin + 2 * pair
+            lead(index + 1, odd)
+            follow(index, even)
+            lead(index + 2, even)
+            follow(index + 1, odd)
+
+        lead(end - 1, odd)
+        follow(end - 2, even)
+        follow(end - 1, odd)
+
+    def edge_lead(index, buffer):
+        place = tile(index)
+        buffer[...] = (
             dot(edges[place, :], ein[own_w, :])
             + dot(pick_rows(send_col[place, :], 0, node_count), from_table[...])
             + dot(pick_rows(recv_col[place, :], 0, node_count), to_table[...])
         )
 
-    loads[EOUT].wait()
-    loads[EGAIN].wait()
-    for copy in halo_copies:
-        copy.wait_recv()
-    halo_table[...] = dot(arrived[...].reshape(halo, width), ein[from_w, :]).astype(BF16)
-
-    @pl.loop(0, edge_count // step_e)
-    def _(index):
-        place = pl.ds(pl.multiple_of(index * step_e, step_e), step_e)
-        value = edge_pre[place, :] + dot(
+    def halo_ready():
+        for copy in halo_copies:
+            copy.wait_recv()
+        halo_table[...] = dot(arrived[...].reshape(halo, width), ein[from_w, :]).astype(BF16)
+
+    def edge_follow(index, buffer):
+        place = tile(index)
+        value = buffer[...] + dot(
             pick_rows(send_col[place, :], node_count, halo), halo_table[...]
         )
         act, slope = swish_pair(value)
@@ -281,6 +327,8 @@
         edge_inv[place, :] = jnp.broadcast_to(inverse, (step_e, LANES))
         edge_mid[place, :] = (normed * egain[...]).astype(BF16)
 
+    pipeline(0, edge_count // step_e, edge_lead, edge_follow, halo_ready)
+
     for index in (NIN, NOUT, NGAIN, NCOT):
         loads[index].wait()
     near = slice(0, width)
@@ -288,13 +336,19 @@
     gains[...] = jnp.zeros_like(gains)
     step_v = tile_of(node_count, (256, 128))
 
-    @pl.loop(0, node_count // step_v)
-    def _(index):
-        start = pl.multiple_of(index * step_v, step_v)
-        place = pl.ds(start, step_v)
-        got = dot(pick_columns(recv_row[...], start, step_v), edge_mid[...]).astype(BF16)
-        gathered[place, :] = got
-        act, slope = swish_pair(dot(nodes[place, :], nin[near, :]) + dot(got, nin[far, :]))
+    def collect(start):
+        gathered[start : start + step_v, :] = dot(
+            pick_columns(recv_row[...], start, step_v), edge_mid[...]
+        ).astype(BF16)
+
+    collect(0)
+    for start in range(0, node_count, step_v):
+        place = slice(start, start + step_v)
+        if start + step_v < node_count:
+            collect(start + step_v)
+        act, slope = swish_pair(
+            dot(nodes[place, :], nin[near, :]) + dot(gathered[place, :], nin[far, :])
+        )
         act = act.astype(BF16)
         node_act[place, :] = act
         normed, inverse = normalize(dot(act, nout[...]))
@@ -311,7 +365,7 @@
     outs = {"ein": ein_out, "eout": eout_out, "nin": nin_out, "nout": nout_out}
     for index, (name, start, wide) in enumerate(plan):
         chunks[name, start] = Chunk(
-            env, mats[name], outs[name], start, wide, refs[index * 8 : (index + 1) * 8]
+            env, mats[name], outs[name], start, wide, refs[index * 10 : (index + 1) * 10]
         )
     half = width // 2
     nout_c, nin_c, eout_c = chunks["nout", 0], chunks["nin", 0], chunks["eout", 0]
@@ -325,20 +379,25 @@
 
     loads[ECOT].wait()
 
-    @pl.loop(0, edge_count // step_e)
-    def _(index):
-        place = pl.ds(pl.multiple_of(index * step_e, step_e), step_e)
-        upstream = ecot[place, :].astype(F32) + dot(
-            pick_rows(recv_col[place, :], 0, node_count), gathered_grad[...]
-        )
+    def back_lead(index, buffer):
+        place = tile(index)
+        buffer[...] = dot(pick_rows(recv_col[place, :], 0, node_count), gathered_grad[...])
+
+    def back_follow(index, buffer):
+        place = tile(index)
+        upstream = ecot[place, :].astype(F32) + buffer[...]
         normed = edge_hat[place, :]
         gains[0:8, :] += fold(upstream * normed)
-        edge_mid[place, :] = norm_back(
-            upstream, egain[...], normed, edge_inv[place, 0:1]
-        ).astype(BF16)
-
-    nout_c.planes()
-    nin_c.planes()
+        post = norm_back(upstream, egain[...], normed, edge_inv[place, 0:1]).astype(BF16)
+        edge_mid[place, :] = post
+        edge_grad[place, :] = (dot_nt(post, eout[...]) * edge_slope[place, :]).astype(BF16)
+
+    blocks = edge_count // step_e
+    pipeline(0, blocks // 2, back_lead, back_follow)
+    nout_c.first()
+    nin_c.first()
+    pipeline(blocks // 2, blocks, back_lead, back_follow)
+
     gains[0:1, :] = jnp.sum(gains[0:8, :], axis=0, keepdims=True)
     gains[1:2, :] = jnp.sum(gains[8:16, :], axis=0, keepdims=True)
     gain_graph_copy = send(
@@ -353,21 +412,46 @@
     gain_copies = [
         send(
             gain_mine, gain_plane.at[step - 1], gain_sem.at[0, step], gain_sem.at[1, step],
-            (env.group, env.layer * planes + lax.rem(env.plane + step, planes)),
+            (env.group, env.base + lax.rem(env.plane + step, planes)),
         )
         for step in range(1, planes)
     ]
 
-    @pl.loop(0, edge_count // step_e)
-    def _(index):
-        place = pl.ds(pl.multiple_of(index * step_e, step_e), step_e)
-        edge_grad[place, :] = (
-            dot_nt(edge_mid[place, :], eout[...]) * edge_slope[place, :]
+    step_s = tile_of(rows_all, (384, 256, 128))
+    step_t = tile_of(node_count, (256, 128))
+
+    def scatter_from(columns):
+        @pl.loop(0, rows_all // step_s)
+        def _(index):
+            start = pl.multiple_of(index * step_s, LANES)
+            sums_from[pl.ds(start, step_s), columns] = dot(
+                pick_columns(send_row[...], start, step_s), edge_grad[:, columns]
+            ).astype(BF16)
+
+    def scatter_to(columns):
+        @pl.loop(0, node_count // step_t)
+        def _(index):
+            start = pl.multiple_of(index * step_t, step_t)
+            sums_to[pl.ds(start, step_t), columns] = dot(
+                pick_columns(recv_row[...], start, step_t), edge_grad[:, columns]
+            ).astype(BF16)
+
+    def edge_in_grads(columns):
+        ein_grad[own_w, columns] = dot_tn(edges[...], edge_grad[:, columns]).astype(BF16)
+        ein_grad[from_w, columns] = (
+            dot_tn(nodes[...], sums_from[0:node_count, columns])
+            + dot_tn(arrived[...].reshape(halo, width), sums_from[node_count:rows_all, columns])
         ).astype(BF16)
-
-    nout_c.layers()
-    nin_c.layers()
-    eout_c.planes()
+        ein_grad[to_w, columns] = dot_tn(nodes[...], sums_to[:, columns]).astype(BF16)
+
+    first, second = slice(0, half), slice(half, width)
+    scatter_from(first)
+    nout_c.second()
+    eout_c.first()
+    scatter_to(first)
+    edge_in_grads(first)
+    ein_c[0].graph()
+
     total = gain_mine[...]
     for step in range(1, planes):
         gain_copies[step - 1].wait_recv()
@@ -381,42 +465,7 @@
         )
         for step in range(1, layers)
     ]
-
-    step_s = tile_of(rows_all, (384, 256, 128))
-    step_t = tile_of(node_count, (256, 128))
-
-    def scatter_from(columns):
-        @pl.loop(0, rows_all // step_s)
-        def _(index):
-            start = pl.multiple_of(index * step_s, LANES)
-            sums_from[pl.ds(start, step_s), columns] = dot(
-                pick_columns(send_row[...], start, step_s), edge_grad[:, columns]
-            ).astype(BF16)
-
-    def scatter_to(columns):
-        @pl.loop(0, node_count // step_t)
-        def _(index):
-            start = pl.multiple_of(index * step_t, step_t)
-            sums_to[pl.ds(start, step_t), columns] = dot(
-                pick_columns(recv_row[...], start, step_t), edge_grad[:, columns]
-            ).astype(BF16)
-
-    def edge_in_grads(columns):
-        ein_grad[own_w, columns] = dot_tn(edges[...], edge_grad[:, columns]).astype(BF16)
-        ein_grad[from_w, columns] = (
-            dot_tn(nodes[...], sums_from[0:node_count, columns])
-            + dot_tn(arrived[...].reshape(halo, width), sums_from[node_count:rows_all, columns])
-        ).astype(BF16)
-        ein_grad[to_w, columns] = dot_tn(nodes[...], sums_to[:, columns]).astype(BF16)
-
-    first, second = slice(0, half), slice(half, width)
-    scatter_from(first)
-    scatter_to(first)
-    edge_in_grads(first)
-    ein_c[0].graph()
-    nout_c.finish()
-    nin_c.finish()
-    eout_c.layers()
+    nin_c.second()
 
     scatter_from(second)
     returning[...] = (
@@ -435,20 +484,23 @@
         for step in range(1, domains)
     ]
     returned[env.dom] = returning[env.dom]
-    ein_c[0].planes()
+    nout_c.along()
+    ein_c[0].first()
+    eout_c.second()
     scatter_to(second)
     edge_in_grads(second)
     ein_c[1].graph()
-    nout_c.place()
-    nin_c.place()
-    eout_c.finish()
-    ein_c[0].layers()
+    nin_c.along()
+    nout_c.finish()
+    ein_c[0].second()
+    eout_c.along()
 
     total = gain_mid[...]
     for step in range(1, layers):
         gain_copies[step - 1].wait_recv()
         total = total + gain_layer[step - 1]
-    gain_out[...] = total
+    share = width // domains
+    gain_out[...] = pltpu.roll(total, lax.rem(width - env.dom * share, width), 1)
 
     def edge_tail(begin, end):
         @pl.loop(begin, end)
@@ -458,12 +510,12 @@
                 ecot[place, :].astype(F32) + dot_nt(edge_grad[place, :], ein[own_w, :])
             ).astype(BF16)
 
-    blocks = edge_count // step_e
     edge_tail(0, blocks // 2)
-    ein_c[1].planes()
-    eout_c.place()
+    ein_c[1].first()
+    nout_c.place()
     edge_tail(blocks // 2, blocks)
-    ein_c[0].finish()
+    ein_c[0].along()
+    nin_c.finish()
 
     for step in range(1, domains):
         back_copies[step - 1].wait_recv()
@@ -492,16 +544,22 @@
 
     blocks = node_count // step_v
     node_tail(0, blocks // 2)
-    ein_c[1].layers()
+    ein_c[1].second()
+    eout_c.finish()
+    nin_c.place()
+    node_tail(blocks // 2, blocks)
+    ein_c[0].finish()
+    ein_c[1].along()
+    eout_c.place()
     ein_c[0].place()
-    node_tail(blocks // 2, blocks)
     ein_c[1].finish()
     ein_c[1].place()
     for copy in sent:
         copy.wait_send()
 
 
-def layer(args, domains, planes, layers):
+def layer(args, domains, side, layers):
+    planes = side * side
     nodes, edges, ncot, ecot, senders, receivers, lists, ein, eout, egain, nin, nout, ngain = args
     node_count, width = nodes.shape
     edge_count = edges.shape[0]
@@ -522,13 +580,13 @@
     inside = pl.BlockSpec(memory_space=pltpu.VMEM)
     share = {name: count // domains for name, count in rows.items()}
     out_shape = (
-        jax.ShapeDtypeStruct((edge_count, width), BF16),
-        jax.ShapeDtypeStruct((node_count, width), BF16),
-        jax.ShapeDtypeStruct((share["ein"], width), F32),
-        jax.ShapeDtypeStruct((share["eout"], width), F32),
-        jax.ShapeDtypeStruct((share["nin"], width), F32),
-        jax.ShapeDtypeStruct((share["nout"], width), F32),
-        jax.ShapeDtypeStruct((8, width), F32),
+        vmem((edge_count, width), BF16),
+        vmem((node_count, width), BF16),
+        vmem((share["ein"], width), F32),
+        vmem((share["eout"], width), F32),
+        vmem((share["nin"], width), F32),
+        vmem((share["nout"], width), F32),
+        vmem((8, width), F32),
     )
     scratch = [vmem(arg.shape, arg.dtype) for arg in args]
     scratch += [
@@ -540,7 +598,8 @@
         vmem((node_count, width), BF16),
         vmem((node_count, width), BF16),
         vmem((halo, width), BF16),
-        vmem((edge_count, width), F32),
+        vmem((256, width), F32),
+        vmem((256, width), F32),
         vmem((edge_count, width), F32),
         vmem((edge_count, width), BF16),
         vmem((edge_count, width), F32),
@@ -575,15 +634,17 @@
         count = share[name]
         scratch += [
             vmem((rows[name], wide), BF16),
-            vmem((layers, planes, count, wide), BF16),
-            vmem((planes - 1, layers, count, wide), BF16),
+            vmem((side, side, layers, count, wide), BF16),
+            vmem((side - 1, side, layers, count, wide), BF16),
+            vmem((side, layers, count, wide), BF16),
+            vmem((side - 1, layers, count, wide), BF16),
             vmem((layers, count, wide), BF16),
             vmem((layers - 1, count, wide), BF16),
             vmem((count, wide), BF16),
             vmem((count, wide), BF16),
-            dma((2, planes + layers)),
+            dma((2, 2 * side + layers - 1)),
         ]
-    shape = (node_count, edge_count, width, domains, slots, planes, layers, plan)
+    shape = (node_count, edge_count, width, domains, slots, side, layers, plan)
     return pl.pallas_call(
         functools.partial(layer_kernel, shape),
         out_shape=out_shape,
@@ -591,10 +652,41 @@
         out_specs=(inside,) * len(out_shape),
         scratch_shapes=scratch,
         compiler_params=pltpu.CompilerParams(
-            collective_id=0, has_side_effects=True, vmem_limit_bytes=63 * 1024 * 1024
+            collective_id=0, has_side_effects=True, vmem_limit_bytes=56 * 1024 * 1024
         ),
         name="layer",
     )(*args)
+
+
+def hand_kernel(*refs):
+    sources, targets, sems = refs[:7], refs[7:15], refs[15]
+    copies = [
+        pltpu.make_async_copy(source, target, sems.at[index])
+        for index, (source, target) in enumerate(zip(sources[:6], targets[:6]))
+    ]
+    for copy in copies:
+        copy.start()
+    gains = sources[6]
+    share = targets[6].shape[1]
+    targets[6][...] = gains[0:1, 0:share]
+    targets[7][...] = gains[1:2, 0:share]
+    for copy in copies:
+        copy.wait()
+
+
+def hand_out(results, share):
+    inside = pl.BlockSpec(memory_space=pltpu.VMEM)
+    anywhere = pl.BlockSpec(memory_space=pl.ANY)
+    return pl.pallas_call(
+        hand_kernel,
+        out_shape=tuple(jax.ShapeDtypeStruct(value.shape, value.dtype) for value in results[:6])
+        + (jax.ShapeDtypeStruct((1, share), F32),) * 2,
+        in_specs=[inside] * 7,
+        out_specs=(anywhere,) * 6 + (inside,) * 2,
+        scratch_shapes=[pltpu.SemaphoreType.DMA((6,))],
+        compiler_params=pltpu.CompilerParams(vmem_limit_bytes=6 * 1024 * 1024),
+        name="hand_out",
+    )(*results)
 
 
 def local(
@@ -602,19 +694,18 @@
     edge_in, edge_out, edge_gain, node_in, node_out, node_gain,
 ):
     domains = lax.axis_size("dom")
-    planes = 1
-    while planes * planes < domains:
-        planes *= 2
+    side = 1
+    while 8 * side**3 <= domains:
+        side *= 2
     width = nodes.shape[2]
     args = (
         nodes[0], edges[0], node_cotangent[0], edge_cotangent[0], senders, receivers,
         send_rows[0].T, edge_in, edge_out, edge_gain[None], node_in, node_out, node_gain[None],
     )
-    results = layer(args, domains, planes, domains // planes)
-    grad_edges, grad_nodes, ein, eout, nin, nout, gains = results
-    share = width // domains
-    own = lax.dynamic_slice_in_dim(gains, lax.axis_index("dom") * share, share, 1)
-    return grad_edges[None], grad_nodes[None], ein, eout, nin, nout, own[0], own[1]
+    results = layer(args, domains, side, domains // (side * side))
+    results = hand_out(results, width // domains)
+    grad_edges, grad_nodes, ein, eout, nin, nout, edge_share, node_share = results
+    return grad_edges[None], grad_nodes[None], ein, eout, nin, nout, edge_share[0], node_share[0]
 
 
 def solution(mesh):

time: 85.6 us -> 71.2 us (0.83)
  local copies, waits for them, and re-layouts: 8.06 us -> 0 us
  Pallas kernels: 76.6 us -> 70.2 us
    pallas_call x1, Pallas kernels: 76.6 us -> 67.8 us  [layer(): pl.pallas_call(functools.partial(layer_kernel, shape), out_shape=out_shap...]
    unnamed x16 -> x0, local copies, waits for them, and re-layouts: 6.79 us -> none
    pallas_call x0 -> x1, Pallas kernels: none -> 2.36 us  [hand_out(): pl.pallas_call(hand_kernel, out_shape=tuple((jax.ShapeDtypeStruct(value.s...]
where the time goes in v1:
time: 71.2 us; the launch traced here: 71 us
  Pallas kernels  70.2 us (99%)
  between operations  0.83 us (1%)
    pallas_call x1, Pallas kernels, layer(): pl.pallas_call(functools.partial(layer_kernel, shape), out_shape=out_shap...  67.8 us
    pallas_call x1, Pallas kernels, hand_out(): pl.pallas_call(hand_kernel, out_shape=tuple((jax.ShapeDtypeStruct(value.s...  2.36 us

profile of v1, /device:TPU:0, one launch (start us, length us, event | category | flops | bytes accessed | tf_op | source)
XLA Modules:
  0.0 71.0 jit_solution(2648408929602444465)
XLA Ops:
  0.6 67.8 %layer.1 = (bf16[2048,512]{1,0:T(8,128)(2,1)S(1)}, bf16[1024,512]{1,0:T(8,128)(2,1)S(1)}, f32[96,512]{1,0:T(8,128)S(1)}, f32[32,512]{1,0:T(8,128)S(1)}, f32[64,5...) custom-call(bf16[1024,512]{1,0:T(8,128)(2,1)} %bitcast.15, bf16[2048,512]{1,0:T(8,128)(2,1)} %bitcast.13, ...), custom_call_target="tpu_custom_call" | custom-call | tf_op jit(solution)/shard_map/layer/pallas_call | solution.py:648
  68.5 2.4 %hand_out.1 = (bf16[2048,512]{1,0:T(8,128)(2,1)}, bf16[1024,512]{1,0:T(8,128)(2,1)}, f32[96,512]{1,0:T(8,128)}, f32[32,512]{1,0:T(8,128)}, f32[64,512]{1,0:T(8,1...) custom-call(bf16[2048,512]{1,0:T(8,128)(2,1)S(1)} %get-tuple-element.23.refs_0_, ...), custom_call_target="tpu_custom_call" | custom-call | tf_op jit(solution)/shard_map/hand_out/pallas_call | solution.py:680

commit v2 on v1

--- a/solution.py
+++ b/solution.py
@@ -71,18 +71,27 @@
 
 
 class Chunk:
-    def __init__(self, env, mat, out, start, wide, refs):
+    def __init__(self, env, mat, out, start, wide, begin, end, refs):
         self.env, self.mat, self.out, self.start, self.wide = env, mat, out, start, wide
+        self.begin, self.end = begin, end
         (
             self.from_graph, self.sum_graph, self.from_first, self.sum_first, self.from_second,
             self.sum_second, self.from_layer, self.total, self.from_other, self.sem,
         ) = refs
         self.slot = 0
-
-    def send(self, src, dst, device):
+        whole = begin == 0 and end == env.layers
+        self.mine = None if whole else self.owned(env.layer)
+        self.whole = whole
+        first_row = begin * env.planes * self.total.shape[0]
+        self.rows = slice(first_row, first_row + self.from_graph.shape[0])
+
+    def owned(self, layer):
+        return jnp.logical_and(layer >= self.begin, layer < self.end)
+
+    def send(self, src, dst, device, when=None):
         slot = self.slot
         self.slot += 1
-        return self.env.send(src, dst, self.sem.at[0, slot], self.sem.at[1, slot], device)
+        return self.env.send(src, dst, self.sem.at[0, slot], self.sem.at[1, slot], device, when)
 
     def columns(self, group):
         return pl.ds(pl.multiple_of(self.start + group * self.wide, LANES), self.wide)
@@ -90,7 +99,7 @@
     def graph(self):
         env = self.env
         self.graph_copy = self.send(
-            self.mat.at[:, self.columns(env.other)], self.from_graph, (env.other, env.dom)
+            self.mat.at[self.rows, self.columns(env.other)], self.from_graph, (env.other, env.dom)
         )
 
     def first(self):
@@ -98,10 +107,11 @@
         side = env.side
         count = self.total.shape[0]
         self.graph_copy.wait_recv()
-        for index in range(env.layers * side * side):
+        for index in range((self.end - self.begin) * side * side):
             x, y, layer = index % side, index // side % side, index // (side * side)
             rows = slice(index * count, (index + 1) * count)
-            value = self.mat[rows, self.columns(env.group)].astype(F32)
+            there = slice(self.rows.start + rows.start, self.rows.start + rows.stop)
+            value = self.mat[there, self.columns(env.group)].astype(F32)
             value = value + self.from_graph[rows, :].astype(F32)
             self.sum_graph[x + env.group * (y - x), y + env.group * (x - y), layer] = value.astype(BF16)
         self.copies = []
@@ -143,28 +153,46 @@
         self.copies = []
         for step in range(1, env.layers):
             target = lax.rem(env.layer + step, env.layers)
+            place = target if self.whole else jnp.clip(target - self.begin, 0, self.end - self.begin - 1)
             self.copies.append(
                 self.send(
-                    self.sum_second.at[target],
+                    self.sum_second.at[place],
                     self.from_layer.at[step - 1],
                     (env.group, target * env.planes + env.plane),
+                    None if self.whole else self.owned(target),
                 )
             )
 
     def finish(self):
         env = self.env
-        value = self.sum_second[env.layer].astype(F32)
-        for step in range(1, env.layers):
-            self.copies[step - 1].wait_recv()
-            value = value + self.from_layer[step - 1].astype(F32)
-        short = value.astype(BF16)
-        self.total[...] = short
-        self.other_copy = self.send(self.total, self.from_other, (env.other, env.dom))
-        self.out[:, self.columns(env.group)] = short.astype(F32)
+
+        def last():
+            place = env.layer - self.begin
+            if not self.whole:
+                place = jnp.clip(place, 0, self.end - self.begin - 1)
+            value = self.sum_second[place].astype(F32)
+            for step in range(1, env.layers):
+                self.copies[step - 1].wait_recv()
+                value = value + self.from_layer[step - 1].astype(F32)
+            short = value.astype(BF16)
+            self.total[...] = short
+            self.out[:, self.columns(env.group)] = short.astype(F32)
+
+        if self.whole:
+            last()
+        else:
+            pl.when(self.mine)(last)
+        self.other_copy = self.send(self.total, self.from_other, (env.other, env.dom), self.mine)
 
     def place(self):
-        self.other_copy.wait_recv()
-        self.out[:, self.columns(self.env.other)] = self.from_other[...].astype(F32)
+        def last():
+            self.other_copy.wait_recv()
+            self.out[:, self.columns(self.env.other)] = self.from_other[...].astype(F32)
+
+        if self.whole:
+            last()
+        else:
+            pl.when(self.mine)(last)
 
 
 class Env:
@@ -184,12 +212,12 @@
     ) = loaded
     (
         send_col, recv_col, list_col, outgoing, arrived, from_table, to_table, halo_table,
-        even, odd, edge_slope, edge_act, edge_hat, edge_inv, edge_mid, edge_grad,
+        even, odd, node_near, edge_slope, edge_act, edge_hat, edge_inv, edge_mid, edge_grad,
         gathered, node_act, node_mid, node_grad, gathered_grad, sums_from, sums_to, returning, returned,
         ein_grad, eout_grad, nin_grad, nout_grad,
         gains, gain_graph, gain_mine, gain_plane, gain_mid, gain_layer,
         load_sem, halo_sem, back_sem, gain_sem,
-    ), refs = refs[:39], refs[39:]
+    ), refs = refs[:40], refs[40:]
 
     env = Env()
     env.group = lax.axis_index("group")
@@ -205,16 +233,27 @@
     env.tail_stride = side - env.group * (side - 1)
     sent = []
 
-    def send(src, dst, send_sem, recv_sem, device):
+    def send(src, dst, send_sem, recv_sem, device, when=None):
         copy = pltpu.make_async_remote_copy(
             src_ref=src, dst_ref=dst, send_sem=send_sem, recv_sem=recv_sem,
             device_id=device, device_id_type=MESH,
         )
-        copy.start()
-        sent.append(copy)
+        if when is None:
+            copy.start()
+        else:
+            pl.when(when)(copy.start)
+        sent.append((copy, when))
         return copy
 
     env.send = send
+
+    def drain():
+        for copy, when in sent:
+            if when is None:
+                copy.wait_send()
+            else:
+                pl.when(when)(copy.wait_send)
+        sent.clear()
 
     def peer(step):
         return lax.rem(env.dom + step, domains)
@@ -224,7 +263,7 @@
         for index, (src, dst) in enumerate(zip(inputs, loaded))
     ]
     NODES, EDGES, NCOT, ECOT, SEND, RECV, LIST, EIN, EOUT, EGAIN, NIN, NOUT, NGAIN = range(13)
-    for index in (LIST, NODES, SEND, RECV, EIN, EDGES, EOUT, EGAIN, NIN, NOUT, NGAIN, NCOT, ECOT):
+    for index in (LIST, SEND, RECV, NODES, EIN, EDGES, EOUT, EGAIN, NIN, NOUT, NGAIN, NCOT, ECOT):
         loads[index].start()
 
     barrier = pltpu.get_barrier_semaphore()
@@ -237,6 +276,14 @@
         list_col[index * slots : (index + 1) * slots, :] = jnp.broadcast_to(
             list_in[:, index : index + 1], (slots, LANES)
         )
+    loads[SEND].wait()
+    loads[RECV].wait()
+
+    for block in range(0, edge_count, LANES):
+        place = slice(block, block + LANES)
+        send_col[place, :] = jnp.transpose(jnp.broadcast_to(send_row[:, place], (LANES, LANES)))
+        recv_col[place, :] = jnp.transpose(jnp.broadcast_to(recv_row[:, place], (LANES, LANES)))
+
     loads[NODES].wait()
     outgoing[...] = (
         dot(pick_rows(list_col[...], 0, node_count), nodes[...])
@@ -256,14 +303,6 @@
     ]
     arrived[env.dom] = outgoing[env.dom]
 
-    loads[SEND].wait()
-    loads[RECV].wait()
-
-    for block in range(0, edge_count, LANES):
-        place = slice(block, block + LANES)
-        send_col[place, :] = jnp.transpose(jnp.broadcast_to(send_row[:, place], (LANES, LANES)))
-        recv_col[place, :] = jnp.transpose(jnp.broadcast_to(recv_row[:, place], (LANES, LANES)))
-
     loads[EIN].wait()
     own_w = slice(0, width)
     from_w = slice(width, 2 * width)
@@ -278,27 +317,13 @@
 
     for index in (EDGES, EOUT, EGAIN):
         loads[index].wait()
-    step_e = tile_of(edge_count, (256, 128))
+    step_e = even.shape[0]
+    blocks = edge_count // step_e
 
     def tile(index):
-        return pl.ds(pl.multiple_of(index * step_e, step_e), step_e)
-
-    def pipeline(begin, end, lead, follow, between=None):
-        lead(begin, even)
-        if between is not None:
-            between()
-
-        @pl.loop(0, (end - begin) // 2 - 1)
-        def _(pair):
-            index = begin + 2 * pair
-            lead(index + 1, odd)
-            follow(index, even)
-            lead(index + 2, even)
-            follow(index + 1, odd)
-
-        lead(end - 1, odd)
-        follow(end - 2, even)
-        follow(end - 1, odd)
+        return slice(index * step_e, (index + 1) * step_e)
+
+    buffers = (even, odd)
 
     def edge_lead(index, buffer):
         place = tile(index)
@@ -327,14 +352,22 @@
         edge_inv[place, :] = jnp.broadcast_to(inverse, (step_e, LANES))
         edge_mid[place, :] = (normed * egain[...]).astype(BF16)
 
-    pipeline(0, edge_count // step_e, edge_lead, edge_follow, halo_ready)
-
-    for index in (NIN, NOUT, NGAIN, NCOT):
-        loads[index].wait()
+    edge_lead(0, buffers[0])
+    edge_lead(1, buffers[1])
+    loads[NIN].wait()
     near = slice(0, width)
     far = slice(width, 2 * width)
+    node_near[...] = dot(nodes[...], nin[near, :])
+    halo_ready()
+    for index in range(blocks):
+        edge_follow(index, buffers[index % 2])
+        if index + 2 < blocks:
+            edge_lead(index + 2, buffers[index % 2])
+
+    for index in (NOUT, NGAIN, NCOT):
+        loads[index].wait()
     gains[...] = jnp.zeros_like(gains)
-    step_v = tile_of(node_count, (256, 128))
+    step_v = tile_of(node_count, (512, 256, 128))
 
     def collect(start):
         gathered[start : start + step_v, :] = dot(
@@ -347,7 +380,7 @@
         if start + step_v < node_count:
             collect(start + step_v)
         act, slope = swish_pair(
-            dot(nodes[place, :], nin[near, :]) + dot(gathered[place, :], nin[far, :])
+            node_near[place, :] + dot(gathered[place, :], nin[far, :])
         )
         act = act.astype(BF16)
         node_act[place, :] = act
@@ -363,13 +396,14 @@
     chunks = {}
     mats = {"ein": ein_grad, "eout": eout_grad, "nin": nin_grad, "nout": nout_grad}
     outs = {"ein": ein_out, "eout": eout_out, "nin": nin_out, "nout": nout_out}
-    for index, (name, start, wide) in enumerate(plan):
-        chunks[name, start] = Chunk(
-            env, mats[name], outs[name], start, wide, refs[index * 10 : (index + 1) * 10]
+    for index, (name, start, wide, begin, end) in enumerate(plan):
+        chunks[name, start, begin] = Chunk(
+            env, mats[name], outs[name], start, wide, begin, end, refs[index * 10 : (index + 1) * 10]
         )
     half = width // 2
-    nout_c, nin_c, eout_c = chunks["nout", 0], chunks["nin", 0], chunks["eout", 0]
-    ein_c = (chunks["ein", 0], chunks["ein", half])
+    nout_c, nin_c, eout_c = (chunks[name, 0, 0] for name in ("nout", "nin", "eout"))
+    low_c = (chunks["ein", 0, 0], chunks["ein", half, 0])
+    high_c = (chunks["ein", 0, layers // 2], chunks["ein", half, layers // 2])
 
     nout_grad[...] = dot_tn(node_act[...], node_mid[...]).astype(BF16)
     nout_c.graph()
@@ -392,11 +426,14 @@
         edge_mid[place, :] = post
         edge_grad[place, :] = (dot_nt(post, eout[...]) * edge_slope[place, :]).astype(BF16)
 
-    blocks = edge_count // step_e
-    pipeline(0, blocks // 2, back_lead, back_follow)
-    nout_c.first()
-    nin_c.first()
-    pipeline(blocks // 2, blocks, back_lead, back_follow)
+    back_lead(0, buffers[0])
+    for index in range(blocks):
+        if index + 1 < blocks:
+            back_lead(index + 1, buffers[(index + 1) % 2])
+        back_follow(index, buffers[index % 2])
+        if index == 0:
+            nout_c.first()
+            nin_c.first()
 
     gains[0:1, :] = jnp.sum(gains[0:8, :], axis=0, keepdims=True)
     gains[1:2, :] = jnp.sum(gains[8:16, :], axis=0, keepdims=True)
@@ -404,26 +441,13 @@
         gains.at[0:8], gain_graph, gain_sem.at[0, 0], gain_sem.at[1, 0], (env.other, env.dom)
     )
 
-    eout_grad[...] = dot_tn(edge_act[...], edge_mid[...]).astype(BF16)
-    eout_c.graph()
-
-    gain_graph_copy.wait_recv()
-    gain_mine[...] = gains[0:8, :] + gain_graph[...]
-    gain_copies = [
-        send(
-            gain_mine, gain_plane.at[step - 1], gain_sem.at[0, step], gain_sem.at[1, step],
-            (env.group, env.base + lax.rem(env.plane + step, planes)),
-        )
-        for step in range(1, planes)
-    ]
-
-    step_s = tile_of(rows_all, (384, 256, 128))
-    step_t = tile_of(node_count, (256, 128))
+    step_s = tile_of(rows_all, (576, 512, 384, 256, 128))
+    step_t = tile_of(node_count, (512, 256, 128))
 
     def scatter_from(columns):
         @pl.loop(0, rows_all // step_s)
         def _(index):
-            start = pl.multiple_of(index * step_s, LANES)
+            start = pl.multiple_of(index * step_s, 64)
             sums_from[pl.ds(start, step_s), columns] = dot(
                 pick_columns(send_row[...], start, step_s), edge_grad[:, columns]
             ).astype(BF16)
@@ -436,22 +460,60 @@
                 pick_columns(recv_row[...], start, step_t), edge_grad[:, columns]
             ).astype(BF16)
 
-    def edge_in_grads(columns):
+    def own_and_from(columns):
         ein_grad[own_w, columns] = dot_tn(edges[...], edge_grad[:, columns]).astype(BF16)
         ein_grad[from_w, columns] = (
             dot_tn(nodes[...], sums_from[0:node_count, columns])
             + dot_tn(arrived[...].reshape(halo, width), sums_from[node_count:rows_all, columns])
         ).astype(BF16)
+
+    def toward(columns):
         ein_grad[to_w, columns] = dot_tn(nodes[...], sums_to[:, columns]).astype(BF16)
 
     first, second = slice(0, half), slice(half, width)
+    eout_grad[...] = dot_tn(edge_act[...], edge_mid[...]).astype(BF16)
+    eout_c.graph()
+    nout_c.second()
+
     scatter_from(first)
-    nout_c.second()
     eout_c.first()
+    gain_graph_copy.wait_recv()
+    gain_mine[...] = gains[0:8, :] + gain_graph[...]
+    gain_copies = [
+        send(
+            gain_mine, gain_plane.at[step - 1], gain_sem.at[0, step], gain_sem.at[1, step],
+            (env.group, env.base + lax.rem(env.plane + step, planes)),
+        )
+        for step in range(1, planes)
+    ]
+    own_and_from(first)
+    low_c[0].graph()
+    nin_c.second()
     scatter_to(first)
-    edge_in_grads(first)
-    ein_c[0].graph()
-
+    low_c[0].first()
+    nout_c.along()
+    toward(first)
+    high_c[0].graph()
+
+    scatter_from(second)
+    returning[...] = (
+        dot_nt(sums_from[node_count:rows_all, :], ein[from_w, :])
+        .astype(BF16)
+        .reshape(domains, slots, width)
+    )
+    back_copies = [
+        send(
+            returning.at[peer(step)],
+            returned.at[env.dom],
+            back_sem.at[0, step - 1],
+            back_sem.at[1, step - 1],
+            (env.group, peer(step)),
+        )
+        for step in range(1, domains)
+    ]
+    returned[env.dom] = returning[env.dom]
+    high_c[0].first()
+    eout_c.second()
     total = gain_mine[...]
     for step in range(1, planes):
         gain_copies[step - 1].wait_recv()
@@ -465,57 +527,27 @@
         )
         for step in range(1, layers)
     ]
-    nin_c.second()
-
-    scatter_from(second)
-    returning[...] = (
-        dot_nt(sums_from[node_count:rows_all, :], ein[from_w, :])
-        .astype(BF16)
-        .reshape(domains, slots, width)
-    )
-    back_copies = [
-        send(
-            returning.at[peer(step)],
-            returned.at[env.dom],
-            back_sem.at[0, step - 1],
-            back_sem.at[1, step - 1],
-            (env.group, peer(step)),
-        )
-        for step in range(1, domains)
-    ]
-    returned[env.dom] = returning[env.dom]
-    nout_c.along()
-    ein_c[0].first()
-    eout_c.second()
+    own_and_from(second)
+    low_c[1].graph()
+    nin_c.along()
     scatter_to(second)
-    edge_in_grads(second)
-    ein_c[1].graph()
-    nin_c.along()
-    nout_c.finish()
-    ein_c[0].second()
+    low_c[1].first()
+    low_c[0].second()
     eout_c.along()
-
-    total = gain_mid[...]
-    for step in range(1, layers):
-        gain_copies[step - 1].wait_recv()
-        total = total + gain_layer[step - 1]
-    share = width // domains
-    gain_out[...] = pltpu.roll(total, lax.rem(width - env.dom * share, width), 1)
+    toward(second)
+    high_c[1].graph()
 
     def edge_tail(begin, end):
-        @pl.loop(begin, end)
-        def _(index):
-            place = pl.ds(pl.multiple_of(index * step_e, step_e), step_e)
+        for index in range(begin, end):
+            place = tile(index)
             edges_out[place, :] = (
                 ecot[place, :].astype(F32) + dot_nt(edge_grad[place, :], ein[own_w, :])
             ).astype(BF16)
 
-    edge_tail(0, blocks // 2)
-    ein_c[1].first()
-    nout_c.place()
-    edge_tail(blocks // 2, blocks)
-    ein_c[0].along()
-    nin_c.finish()
+    edge_tail(0, blocks)
+    high_c[1].first()
+    high_c[0].second()
+    low_c[0].along()
 
     for step in range(1, domains):
         back_copies[step - 1].wait_recv()
@@ -530,10 +562,8 @@
     back = returned[...].reshape(halo, width)
 
     def node_tail(begin, end):
-        @pl.loop(begin, end)
-        def _(index):
-            start = pl.multiple_of(index * step_v, step_v)
-            place = pl.ds(start, step_v)
+        for start in range(begin * step_v, end * step_v, step_v):
+            place = slice(start, start + step_v)
             nodes_out[place, :] = (
                 ncot[place, :].astype(F32)
                 + dot_nt(node_grad[place, :], nin[near, :])
@@ -544,18 +574,33 @@
 
     blocks = node_count // step_v
     node_tail(0, blocks // 2)
-    ein_c[1].second()
+    low_c[1].second()
+    nout_c.finish()
+    node_tail(blocks // 2, blocks)
+    high_c[0].along()
+    high_c[1].second()
+    low_c[1].along()
+    nin_c.finish()
+    total = gain_mid[...]
+    for step in range(1, layers):
+        gain_copies[step - 1].wait_recv()
+        total = total + gain_layer[step - 1]
+    share = width // domains
+    gain_out[...] = pltpu.roll(total, lax.rem(width - env.dom * share, width), 1)
+    nout_c.place()
     eout_c.finish()
+    high_c[1].along()
+    low_c[0].finish()
     nin_c.place()
-    node_tail(blocks // 2, blocks)
-    ein_c[0].finish()
-    ein_c[1].along()
+    high_c[0].finish()
     eout_c.place()
-    ein_c[0].place()
-    ein_c[1].finish()
-    ein_c[1].place()
-    for copy in sent:
-        copy.wait_send()
+    low_c[1].finish()
+    low_c[0].place()
+    high_c[0].place()
+    high_c[1].finish()
+    low_c[1].place()
+    high_c[1].place()
+    drain()
 
 
 def layer(args, domains, side, layers):
@@ -566,12 +611,15 @@
     slots = lists.shape[0]
     halo = domains * slots
     half = width // 2
+    tile = tile_of(edge_count // 4, (512, 256, 128))
     plan = (
-        ("nout", 0, half),
-        ("nin", 0, half),
-        ("eout", 0, half),
-        ("ein", 0, half // 2),
-        ("ein", half, half // 2),
+        ("nout", 0, half, 0, layers),
+        ("nin", 0, half, 0, layers),
+        ("eout", 0, half, 0, layers),
+        ("ein", 0, half // 2, 0, layers // 2),
+        ("ein", 0, half // 2, layers // 2, layers),
+        ("ein", half, half // 2, 0, layers // 2),
+        ("ein", half, half // 2, layers // 2, layers),
     )
     rows = {"ein": 3 * width, "eout": width, "nin": 2 * width, "nout": width}
     dma = pltpu.SemaphoreType.DMA
@@ -598,8 +646,9 @@
         vmem((node_count, width), BF16),
         vmem((node_count, width), BF16),
         vmem((halo, width), BF16),
-        vmem((256, width), F32),
-        vmem((256, width), F32),
+        vmem((tile, width), F32),
+        vmem((tile, width), F32),
+        vmem((node_count, width), F32),
         vmem((edge_count, width), F32),
         vmem((edge_count, width), BF16),
         vmem((edge_count, width), F32),
@@ -630,15 +679,16 @@
         dma((2, domains - 1)),
         dma((2, planes + layers - 1)),
     ]
-    for name, _, wide in plan:
+    for name, _, wide, begin, end in plan:
         count = share[name]
+        some = end - begin
         scratch += [
-            vmem((rows[name], wide), BF16),
-            vmem((side, side, layers, count, wide), BF16),
-            vmem((side - 1, side, layers, count, wide), BF16),
-            vmem((side, layers, count, wide), BF16),
-            vmem((side - 1, layers, count, wide), BF16),
-            vmem((layers, count, wide), BF16),
+            vmem((some * planes * count, wide), BF16),
+            vmem((side, side, some, count, wide), BF16),
+            vmem((side - 1, side, some, count, wide), BF16),
+            vmem((side, some, count, wide), BF16),
+            vmem((side - 1, some, count, wide), BF16),
+            vmem((some, count, wide), BF16),
             vmem((layers - 1, count, wide), BF16),
             vmem((count, wide), BF16),
             vmem((count, wide), BF16),
@@ -659,17 +709,16 @@
 
 
 def hand_kernel(*refs):
-    sources, targets, sems = refs[:7], refs[7:15], refs[15]
+    sources, targets, shares, sems = refs[:7], refs[7:15], refs[15:17], refs[17]
+    share = shares[0].shape[1]
+    for row in range(2):
+        shares[row][...] = sources[6][row : row + 1, 0:share]
     copies = [
         pltpu.make_async_copy(source, target, sems.at[index])
-        for index, (source, target) in enumerate(zip(sources[:6], targets[:6]))
+        for index, (source, target) in enumerate(zip(sources[:6] + shares, targets))
     ]
     for copy in copies:
         copy.start()
-    gains = sources[6]
-    share = targets[6].shape[1]
-    targets[6][...] = gains[0:1, 0:share]
-    targets[7][...] = gains[1:2, 0:share]
     for copy in copies:
         copy.wait()
 
@@ -682,8 +731,8 @@
         out_shape=tuple(jax.ShapeDtypeStruct(value.shape, value.dtype) for value in results[:6])
         + (jax.ShapeDtypeStruct((1, share), F32),) * 2,
         in_specs=[inside] * 7,
-        out_specs=(anywhere,) * 6 + (inside,) * 2,
-        scratch_shapes=[pltpu.SemaphoreType.DMA((6,))],
+        out_specs=(anywhere,) * 8,
+        scratch_shapes=[pltpu.VMEM((1, share), F32), pltpu.VMEM((1, share), F32), pltpu.SemaphoreType.DMA((8,))],
         compiler_params=pltpu.CompilerParams(vmem_limit_bytes=6 * 1024 * 1024),
         name="hand_out",
     )(*results)

time: 71.2 us -> 60 us (0.84)
  Pallas kernels: 70.2 us -> 59 us
    pallas_call x1, Pallas kernels: 67.8 us -> 57.1 us  [layer(): pl.pallas_call(functools.partial(layer_kernel, shape), out_shape=out_shap...]
where the time goes in v2:
time: 60 us; the launch traced here: 59.8 us
  Pallas kernels  59 us (98%)
  between operations  0.83 us (1%)
    pallas_call x1, Pallas kernels, layer(): pl.pallas_call(functools.partial(layer_kernel, shape), out_shape=out_shap...  57.1 us
    pallas_call x1, Pallas kernels, hand_out(): pl.pallas_call(hand_kernel, out_shape=tuple((jax.ShapeDtypeStruct(value.s...  1.87 us

profile of v2, /device:TPU:0, one launch (start us, length us, event | category | flops | bytes accessed | tf_op | source)
XLA Modules:
  0.0 59.8 jit_solution(5629620754828062368)
XLA Ops:
  0.6 57.1 %layer.1 = (bf16[2048,512]{1,0:T(8,128)(2,1)S(1)}, bf16[1024,512]{1,0:T(8,128)(2,1)S(1)}, f32[96,512]{1,0:T(8,128)S(1)}, f32[32,512]{1,0:T(8,128)S(1)}, f32[64,5...) custom-call(bf16[1024,512]{1,0:T(8,128)(2,1)} %bitcast.15, bf16[2048,512]{1,0:T(8,128)(2,1)} %bitcast.13, ...), custom_call_target="tpu_custom_call" | custom-call | tf_op jit(solution)/shard_map/layer/pallas_call | solution.py:698
  57.8 1.9 %hand_out.1 = (bf16[2048,512]{1,0:T(8,128)(2,1)}, bf16[1024,512]{1,0:T(8,128)(2,1)}, f32[96,512]{1,0:T(8,128)}, f32[32,512]{1,0:T(8,128)}, f32[64,512]{1,0:T(8,1...) custom-call(bf16[2048,512]{1,0:T(8,128)(2,1)S(1)} %get-tuple-element.23.refs_0_, ...), custom_call_target="tpu_custom_call" | custom-call | tf_op jit(solution)/shard_map/hand_out/pallas_call | solution.py:729

commit v3 on v2

--- a/solution.py
+++ b/solution.py
@@ -212,12 +212,12 @@
     ) = loaded
     (
         send_col, recv_col, list_col, outgoing, arrived, from_table, to_table, halo_table,
-        even, odd, node_near, edge_slope, edge_act, edge_hat, edge_inv, edge_mid, edge_grad,
+        even, odd, third, node_near, edge_slope, edge_act, edge_hat, edge_inv, edge_mid, edge_grad,
         gathered, node_act, node_mid, node_grad, gathered_grad, sums_from, sums_to, returning, returned,
         ein_grad, eout_grad, nin_grad, nout_grad,
-        gains, gain_graph, gain_mine, gain_plane, gain_mid, gain_layer,
+        gains, gain_sum, gain_graph, gain_mine, gain_plane, gain_mid, gain_layer,
         load_sem, halo_sem, back_sem, gain_sem,
-    ), refs = refs[:40], refs[40:]
+    ), refs = refs[:42], refs[42:]
 
     env = Env()
     env.group = lax.axis_index("group")
@@ -258,6 +258,11 @@
     def peer(step):
         return lax.rem(env.dom + step, domains)
 
+    barrier = pltpu.get_barrier_semaphore()
+    pl.semaphore_signal(barrier, inc=1, device_id=(env.other, env.dom), device_id_type=MESH)
+    for step in range(1, domains):
+        pl.semaphore_signal(barrier, inc=1, device_id=(env.group, peer(step)), device_id_type=MESH)
+
     loads = [
         pltpu.make_async_copy(src, dst, load_sem.at[index])
         for index, (src, dst) in enumerate(zip(inputs, loaded))
@@ -265,11 +270,6 @@
     NODES, EDGES, NCOT, ECOT, SEND, RECV, LIST, EIN, EOUT, EGAIN, NIN, NOUT, NGAIN = range(13)
     for index in (LIST, SEND, RECV, NODES, EIN, EDGES, EOUT, EGAIN, NIN, NOUT, NGAIN, NCOT, ECOT):
         loads[index].start()
-
-    barrier = pltpu.get_barrier_semaphore()
-    pl.semaphore_signal(barrier, inc=1, device_id=(env.other, env.dom), device_id_type=MESH)
-    for step in range(1, domains):
-        pl.semaphore_signal(barrier, inc=1, device_id=(env.group, peer(step)), device_id_type=MESH)
 
     loads[LIST].wait()
     for index in range(domains):
@@ -323,7 +323,7 @@
     def tile(index):
         return slice(index * step_e, (index + 1) * step_e)
 
-    buffers = (even, odd)
+    buffers = (even, odd, third)
 
     def edge_lead(index, buffer):
         place = tile(index)
@@ -352,17 +352,17 @@
         edge_inv[place, :] = jnp.broadcast_to(inverse, (step_e, LANES))
         edge_mid[place, :] = (normed * egain[...]).astype(BF16)
 
-    edge_lead(0, buffers[0])
-    edge_lead(1, buffers[1])
+    for index in range(3):
+        edge_lead(index, buffers[index])
     loads[NIN].wait()
     near = slice(0, width)
     far = slice(width, 2 * width)
     node_near[...] = dot(nodes[...], nin[near, :])
     halo_ready()
     for index in range(blocks):
-        edge_follow(index, buffers[index % 2])
-        if index + 2 < blocks:
-            edge_lead(index + 2, buffers[index % 2])
+        edge_follow(index, buffers[index % 3])
+        if index + 3 < blocks:
+            edge_lead(index + 3, buffers[index % 3])
 
     for index in (NOUT, NGAIN, NCOT):
         loads[index].wait()
@@ -409,7 +409,6 @@
     nout_c.graph()
     nin_grad[near, :] = dot_tn(nodes[...], node_grad[...]).astype(BF16)
     nin_grad[far, :] = dot_tn(gathered[...], node_grad[...]).astype(BF16)
-    nin_c.graph()
 
     loads[ECOT].wait()
 
@@ -427,6 +426,7 @@
         edge_grad[place, :] = (dot_nt(post, eout[...]) * edge_slope[place, :]).astype(BF16)
 
     back_lead(0, buffers[0])
+    nin_c.graph()
     for index in range(blocks):
         if index + 1 < blocks:
             back_lead(index + 1, buffers[(index + 1) % 2])
@@ -435,12 +435,6 @@
             nout_c.first()
             nin_c.first()
 
-    gains[0:1, :] = jnp.sum(gains[0:8, :], axis=0, keepdims=True)
-    gains[1:2, :] = jnp.sum(gains[8:16, :], axis=0, keepdims=True)
-    gain_graph_copy = send(
-        gains.at[0:8], gain_graph, gain_sem.at[0, 0], gain_sem.at[1, 0], (env.other, env.dom)
-    )
-
     step_s = tile_of(rows_all, (576, 512, 384, 256, 128))
     step_t = tile_of(node_count, (512, 256, 128))
 
@@ -473,12 +467,19 @@
     first, second = slice(0, half), slice(half, width)
     eout_grad[...] = dot_tn(edge_act[...], edge_mid[...]).astype(BF16)
     eout_c.graph()
+    gain_sum[0:1, :] = jnp.sum(gains[0:8, :], axis=0, keepdims=True)
+    gain_sum[1:2, :] = jnp.sum(gains[8:16, :], axis=0, keepdims=True)
+    gain_graph_copy = send(
+        gain_sum, gain_graph, gain_sem.at[0, 0], gain_sem.at[1, 0], (env.other, env.dom)
+    )
     nout_c.second()
 
     scatter_from(first)
+    own_and_from(first)
+    low_c[0].graph()
     eout_c.first()
     gain_graph_copy.wait_recv()
-    gain_mine[...] = gains[0:8, :] + gain_graph[...]
+    gain_mine[...] = gain_sum[...] + gain_graph[...]
     gain_copies = [
         send(
             gain_mine, gain_plane.at[step - 1], gain_sem.at[0, step], gain_sem.at[1, step],
@@ -486,14 +487,11 @@
         )
         for step in range(1, planes)
     ]
-    own_and_from(first)
-    low_c[0].graph()
-    nin_c.second()
     scatter_to(first)
-    low_c[0].first()
-    nout_c.along()
     toward(first)
     high_c[0].graph()
+    low_c[0].first()
+    nin_c.second()
 
     scatter_from(second)
     returning[...] = (
@@ -513,6 +511,9 @@
     ]
     returned[env.dom] = returning[env.dom]
     high_c[0].first()
+    nout_c.along()
+    own_and_from(second)
+    low_c[1].graph()
     eout_c.second()
     total = gain_mine[...]
     for step in range(1, planes):
@@ -527,15 +528,12 @@
         )
         for step in range(1, layers)
     ]
-    own_and_from(second)
-    low_c[1].graph()
-    nin_c.along()
     scatter_to(second)
+    toward(second)
+    high_c[1].graph()
     low_c[1].first()
     low_c[0].second()
-    eout_c.along()
-    toward(second)
-    high_c[1].graph()
+    nin_c.along()
 
     def edge_tail(begin, end):
         for index in range(begin, end):
@@ -544,14 +542,28 @@
                 ecot[place, :].astype(F32) + dot_nt(edge_grad[place, :], ein[own_w, :])
             ).astype(BF16)
 
+    def node_tail(start):
+        place = slice(start, start + step_v)
+        node_near[place, :] = (
+            ncot[place, :].astype(F32)
+            + dot_nt(node_grad[place, :], nin[near, :])
+            + dot_nt(sums_from[place, :], ein[from_w, :])
+            + dot_nt(sums_to[place, :], ein[to_w, :])
+        )
+
     edge_tail(0, blocks)
     high_c[1].first()
     high_c[0].second()
+    for start in range(0, node_count // 2, step_v):
+        node_tail(start)
+    eout_c.along()
+    for start in range(node_count // 2, node_count, step_v):
+        node_tail(start)
     low_c[0].along()
+    low_c[1].second()
 
     for step in range(1, domains):
         back_copies[step - 1].wait_recv()
-
     list_row = jnp.concatenate(
         [
             jnp.transpose(list_col[block : block + LANES, :])[0:1, :]
@@ -560,26 +572,17 @@
         axis=1,
     )
     back = returned[...].reshape(halo, width)
-
-    def node_tail(begin, end):
-        for start in range(begin * step_v, end * step_v, step_v):
-            place = slice(start, start + step_v)
-            nodes_out[place, :] = (
-                ncot[place, :].astype(F32)
-                + dot_nt(node_grad[place, :], nin[near, :])
-                + dot_nt(sums_from[place, :], ein[from_w, :])
-                + dot_nt(sums_to[place, :], ein[to_w, :])
-                + dot(pick_columns(list_row, start, step_v), back)
-            ).astype(BF16)
-
-    blocks = node_count // step_v
-    node_tail(0, blocks // 2)
-    low_c[1].second()
+    for start in range(0, node_count, step_v):
+        place = slice(start, start + step_v)
+        nodes_out[place, :] = (
+            node_near[place, :] + dot(pick_columns(list_row, start, step_v), back)
+        ).astype(BF16)
+
+    high_c[1].second()
+    high_c[0].along()
+    low_c[1].along()
+    high_c[1].along()
     nout_c.finish()
-    node_tail(blocks // 2, blocks)
-    high_c[0].along()
-    high_c[1].second()
-    low_c[1].along()
     nin_c.finish()
     total = gain_mid[...]
     for step in range(1, layers):
@@ -587,9 +590,8 @@
         total = total + gain_layer[step - 1]
     share = width // domains
     gain_out[...] = pltpu.roll(total, lax.rem(width - env.dom * share, width), 1)
+    eout_c.finish()
     nout_c.place()
-    eout_c.finish()
-    high_c[1].along()
     low_c[0].finish()
     nin_c.place()
     high_c[0].finish()
@@ -634,7 +636,7 @@
         vmem((share["eout"], width), F32),
         vmem((share["nin"], width), F32),
         vmem((share["nout"], width), F32),
-        vmem((8, width), F32),
+        vmem((2, width), F32),
     )
     scratch = [vmem(arg.shape, arg.dtype) for arg in args]
     scratch += [
@@ -646,6 +648,7 @@
         vmem((node_count, width), BF16),
         vmem((node_count, width), BF16),
         vmem((halo, width), BF16),
+        vmem((tile, width), F32),
         vmem((tile, width), F32),
         vmem((tile, width), F32),
         vmem((node_count, width), F32),
@@ -669,11 +672,12 @@
         vmem((2 * width, width), BF16),
         vmem((width, width), BF16),
         vmem((16, width), F32),
-        vmem((8, width), F32),
-        vmem((8, width), F32),
-        vmem((planes - 1, 8, width), F32),
-        vmem((8, width), F32),
-        vmem((layers - 1, 8, width), F32),
+        vmem((2, width), F32),
+        vmem((2, width), F32),
+        vmem((2, width), F32),
+        vmem((planes - 1, 2, width), F32),
+        vmem((2, width), F32),
+        vmem((layers - 1, 2, width), F32),
         dma((13,)),
         dma((2, domains - 1)),
         dma((2, domains - 1)),

time: 60 us -> 58.5 us (0.975)
  Pallas kernels: 59 us -> 57.5 us
    pallas_call x1, Pallas kernels: 57.1 us -> 55.6 us  [layer(): pl.pallas_call(functools.partial(layer_kernel, shape), out_shape=out_shap...]
where the time goes in v3:
time: 58.5 us; the launch traced here: 58.3 us
  Pallas kernels  57.5 us (98%)
  between operations  0.83 us (1%)
    pallas_call x1, Pallas kernels, layer(): pl.pallas_call(functools.partial(layer_kernel, shape), out_shape=out_shap...  55.6 us
    pallas_call x1, Pallas kernels, hand_out(): pl.pallas_call(hand_kernel, out_shape=tuple((jax.ShapeDtypeStruct(value.s...  1.87 us

profile of v3, /device:TPU:0, one launch (start us, length us, event | category | flops | bytes accessed | tf_op | source)
XLA Modules:
  0.0 58.3 jit_solution(9635737702381844863)
XLA Ops:
  0.6 55.6 %layer.1 = (bf16[2048,512]{1,0:T(8,128)(2,1)S(1)}, bf16[1024,512]{1,0:T(8,128)(2,1)S(1)}, f32[96,512]{1,0:T(8,128)S(1)}, f32[32,512]{1,0:T(8,128)S(1)}, f32[64,5...) custom-call(bf16[1024,512]{1,0:T(8,128)(2,1)} %bitcast.15, bf16[2048,512]{1,0:T(8,128)(2,1)} %bitcast.13, ...), custom_call_target="tpu_custom_call" | custom-call | tf_op jit(solution)/shard_map/layer/pallas_call | solution.py:702
  56.3 1.9 %hand_out.1 = (bf16[2048,512]{1,0:T(8,128)(2,1)}, bf16[1024,512]{1,0:T(8,128)(2,1)}, f32[96,512]{1,0:T(8,128)}, f32[32,512]{1,0:T(8,128)}, f32[64,512]{1,0:T(8,1...) custom-call(bf16[2048,512]{1,0:T(8,128)(2,1)S(1)} %get-tuple-element.23.refs_0_, ...), custom_call_target="tpu_custom_call" | custom-call | tf_op jit(solution)/shard_map/hand_out/pallas_call | solution.py:733

commit v4 on v3

--- a/solution.py
+++ b/solution.py
@@ -309,9 +309,8 @@
     to_w = slice(2 * width, 3 * width)
     step_n = tile_of(node_count, (512, 256, 128))
 
-    @pl.loop(0, node_count // step_n)
-    def _(index):
-        place = pl.ds(pl.multiple_of(index * step_n, step_n), step_n)
+    for start in range(0, node_count, step_n):
+        place = slice(start, start + step_n)
         from_table[place, :] = dot(nodes[place, :], ein[from_w, :]).astype(BF16)
         to_table[place, :] = dot(nodes[place, :], ein[to_w, :]).astype(BF16)
 

time: 58.5 us -> 58.4 us (level)
  no operation moved by 1% of the time
where the time goes in v4:
time: 58.4 us; the launch traced here: 58.2 us
  Pallas kernels  57.4 us (98%)
  between operations  0.83 us (1%)
    pallas_call x1, Pallas kernels, layer(): pl.pallas_call(functools.partial(layer_kernel, shape), out_shape=out_shap...  55.5 us
    pallas_call x1, Pallas kernels, hand_out(): pl.pallas_call(hand_kernel, out_shape=tuple((jax.ShapeDtypeStruct(value.s...  1.87 us

profile of v4, /device:TPU:0, one launch (start us, length us, event | category | flops | bytes accessed | tf_op | source)
XLA Modules:
  0.0 58.2 jit_solution(9829185723868311367)
XLA Ops:
  0.6 55.5 %layer.1 = (bf16[2048,512]{1,0:T(8,128)(2,1)S(1)}, bf16[1024,512]{1,0:T(8,128)(2,1)S(1)}, f32[96,512]{1,0:T(8,128)S(1)}, f32[32,512]{1,0:T(8,128)S(1)}, f32[64,5...) custom-call(bf16[1024,512]{1,0:T(8,128)(2,1)} %bitcast.15, bf16[2048,512]{1,0:T(8,128)(2,1)} %bitcast.13, ...), custom_call_target="tpu_custom_call" | custom-call | tf_op jit(solution)/shard_map/layer/pallas_call | solution.py:701
  56.1 1.9 %hand_out.1 = (bf16[2048,512]{1,0:T(8,128)(2,1)}, bf16[1024,512]{1,0:T(8,128)(2,1)}, f32[96,512]{1,0:T(8,128)}, f32[32,512]{1,0:T(8,128)}, f32[64,512]{1,0:T(8,1...) custom-call(bf16[2048,512]{1,0:T(8,128)(2,1)S(1)} %get-tuple-element.23.refs_0_, ...), custom_call_target="tpu_custom_call" | custom-call | tf_op jit(solution)/shard_map/hand_out/pallas_call | solution.py:732
